TPU v7x, 32 devices: a whole 2x2x4 slice. The times are simulated.
32 devices in a mesh: vocab: 8 (over z, y), batch: 4 (over x, core).
Axes of the slice: x: 2, y: 2, z: 4, core: 2. Of those that a mesh axis runs over, the one named last changes fastest.
Arguments:
- latent_state_rows: bfloat16 [64, 8192], P('batch', 'vocab'), may hold values from -90 to 90
- closing_rescale_coeffs: bfloat16 [8192], replicated, may hold values from 0.5 to 1.5
- output_projection_matrix: bfloat16 [8192, 131072], P(None, ('vocab', 'batch')), may hold values from -3.7565048 to 3.7565048
- config_heat_values: float32 [16], replicated, may hold values from 0.7 to 1.4
- sequence_config_choice: int32 [64], replicated, may hold values from 0 to 15
- ranked_choice_ids: int32 [64, 128], replicated, may hold values from 0 to 131071
- keep_count: int32 [64], replicated, may hold values from 2 to 128
Outputs:
- log_norm: float32 [64], P('batch')
- kept_mass: float32 [64], P('batch')
- renormed: float32 [64, 128], P('batch')
All inputs are finite; a program needn't handle non-finite values.
Results may differ from a plain program's by a relative error of at most 0.0048.
Values may be sent and summed in bfloat16 or wider, within the bound.
A program may use at most 128 MiB of HBM per device.

v0:
```python
import functools

import jax
import jax.numpy as jnp
from jax import lax
from jax.experimental import pallas as pl
from jax.experimental.pallas import tpu as pltpu
from jax.sharding import PartitionSpec as P

MESH = pl.DeviceIdType.MESH
epsilon = 1e-06
LANES = 128
STAT_ROWS = 8
CHUNK_ROWS = 512
STREAM_BYTES = 48 * 1024 * 1024


def iota(shape, axis):
    return lax.broadcasted_iota(jnp.int32, shape, axis)


def column_to_row(column):
    rows = column.shape[0]
    diagonal = iota((rows, LANES), 0) == iota((rows, LANES), 1)
    return jnp.sum(jnp.where(diagonal, column, 0.0), axis=0, keepdims=True)


def row_to_column(row, first, rows):
    width = row.shape[1]
    diagonal = iota((rows, width), 0) + first == iota((rows, width), 1)
    return jnp.sum(jnp.where(diagonal, row, 0.0), axis=1, keepdims=True)


def combine(parts, group):
    candidates = parts[0][:group, :]
    top = parts[0][group : group + 1, :]
    for part in parts[1:]:
        candidates = candidates + part[:group, :]
        top = jnp.maximum(top, part[group : group + 1, :])
    total = jnp.zeros_like(top)
    for part in parts:
        total = total + part[group + 1 : group + 2, :] * jnp.exp(
            part[group : group + 1, :] - top
        )
    return candidates, top, total


def kernel(
    n_v,
    n_b,
    n_slots,
    kc,
    x_ref,
    gain_ref,
    w_ref,
    heat_ref,
    choice_ref,
    ids_ref,
    keep_ref,
    norm_ref,
    mass_ref,
    renorm_ref,
    wbuf,
    xbuf,
    lhs,
    acc,
    outbox,
    inbox,
    midbox,
    lastbox,
    w_sem,
    x_recv,
    a_send,
    x_send,
    c_send,
    t_send,
    t_recv,
    u_send,
    u_recv,
):
    v = lax.axis_index("vocab")
    b = lax.axis_index("batch")
    n_x = n_b // 2
    x = b // 2
    c = b % 2
    partner = 2 * x + (1 - c)
    group, fpd = x_ref.shape
    slots = n_b * group
    depth, cols = w_ref.shape
    n_k = depth // kc
    per_block = fpd // kc

    def stream(k):
        slot = lax.rem(k, n_slots)
        return pltpu.make_async_copy(
            w_ref.at[pl.ds(pl.multiple_of(k * kc, kc), kc), :], wbuf.at[slot], w_sem.at[slot]
        )

    for k in range(n_slots):
        stream(k).start()

    barrier = pltpu.get_barrier_semaphore()
    for j in range(1, n_v):
        pl.semaphore_signal(barrier, inc=1, device_id=((v + j) % n_v, b), device_id_type=MESH)
    for j in range(1, n_b):
        pl.semaphore_signal(barrier, inc=1, device_id=(v, (b + j) % n_b), device_id_type=MESH)
    pl.semaphore_wait(barrier, n_v - 1 + n_b - 1)

    def send(src, dst, send_sem, recv_sem, to):
        copy = pltpu.make_async_remote_copy(
            src_ref=src,
            dst_ref=dst,
            send_sem=send_sem,
            recv_sem=recv_sem,
            device_id=to,
            device_id_type=MESH,
        )
        copy.start()
        return copy

    def arrived(row, col):
        pltpu.make_async_copy(x_ref, xbuf.at[row, col], x_recv.at[row, col]).wait()

    sent = []
    for j in range(1, n_v):
        sent.append(
            send(x_ref, xbuf.at[b, v], a_send.at[j], x_recv.at[b, v], ((v + j) % n_v, b))
        )
    for j in range(n_v):
        origin = (v - j + n_v) % n_v
        block = x_ref if j == 0 else xbuf.at[b, origin]
        if j > 0:
            arrived(b, origin)
        for i in range(1, n_x):
            to = 2 * ((x + i) % n_x) + c
            sent.append(
                send(block, xbuf.at[b, origin], x_send.at[i, j], x_recv.at[b, origin], (v, to))
            )
        sent.append(
            send(block, xbuf.at[b, origin], c_send.at[0, j], x_recv.at[b, origin], (v, partner))
        )
    for j in range(n_v):
        for i in range(1, n_x):
            origin = (v - j + n_v) % n_v
            source = 2 * ((x - i + n_x) % n_x) + c
            arrived(source, origin)
            block = xbuf.at[source, origin]
            sent.append(
                send(block, block, c_send.at[i, j], x_recv.at[source, origin], (v, partner))
            )
    for j in range(n_v):
        for i in range(n_x):
            origin = (v - j + n_v) % n_v
            source = 2 * ((x - i + n_x) % n_x) + (1 - c)
            arrived(source, origin)
    xbuf[b, v] = x_ref[...]

    def square(f, carry):
        values = xbuf[:, f].reshape(slots, fpd).astype(jnp.float32)
        values = values * values
        for t in range(fpd // LANES):
            carry = carry + values[:, t * LANES : (t + 1) * LANES]
        return carry

    squares = lax.fori_loop(0, n_v, square, jnp.zeros((slots, LANES), jnp.float32))
    mean_square = jnp.sum(squares, axis=1, keepdims=True) / depth
    factor = lax.rsqrt(mean_square + epsilon)

    def rescale(f, carry):
        values = xbuf[:, f].reshape(slots, fpd).astype(jnp.float32)
        gain = gain_ref[pl.ds(f, 1), :]
        normed = (values * factor * gain).astype(jnp.bfloat16)
        for i in range(per_block):
            lhs[f * per_block + i] = normed[:, i * kc : (i + 1) * kc]
        return carry

    lax.fori_loop(0, n_v, rescale, 0)

    acc[...] = jnp.zeros_like(acc)

    def multiply(k, carry):
        slot = lax.rem(k, n_slots)
        stream(k).wait()
        acc[...] += jnp.dot(lhs[k], wbuf[slot], preferred_element_type=jnp.float32)

        @pl.when(k + n_slots < n_k)
        def _():
            stream(k + n_slots).start()

        return carry

    lax.fori_loop(0, n_k, multiply, 0)

    choice = row_to_column(choice_ref[...].astype(jnp.float32), 0, slots)
    n_heat = heat_ref.shape[1]
    member = choice == iota((slots, n_heat), 1).astype(jnp.float32)
    heat = jnp.sum(jnp.where(member, heat_ref[...], 0.0), axis=1, keepdims=True)

    local_ids = ids_ref[...] - (v * n_b + b) * cols
    tile_of = local_ids >> 7
    lane_of = local_ids & (LANES - 1)
    picked = jnp.zeros((slots, LANES), jnp.float32)
    top = jnp.full((slots, LANES), -3e38, jnp.float32)
    for t in range(cols // LANES):
        part = acc[:, t * LANES : (t + 1) * LANES] / heat
        acc[:, t * LANES : (t + 1) * LANES] = part
        top = jnp.maximum(top, part)
        found = jnp.take_along_axis(part, lane_of, axis=1, mode="promise_in_bounds")
        picked = jnp.where(tile_of == t, found, picked)
    top = jnp.max(top, axis=1, keepdims=True)
    total = jnp.zeros((slots, LANES), jnp.float32)
    for t in range(cols // LANES):
        total = total + jnp.exp(acc[:, t * LANES : (t + 1) * LANES] - top)
    total = jnp.sum(total, axis=1, keepdims=True)

    for p in range(n_b):
        rows = slice(p * group, (p + 1) * group)
        outbox[p, :group, :] = picked[rows, :]
        outbox[p, group : group + 1, :] = column_to_row(top[rows, :])
        outbox[p, group + 1 : group + 2, :] = column_to_row(total[rows, :])
        outbox[p, group + 2 :, :] = jnp.zeros((STAT_ROWS - 2, LANES), jnp.float32)
    for j in range(1, n_b):
        to = (b + j) % n_b
        sent.append(send(outbox.at[to], inbox.at[b], t_send.at[j], t_recv.at[b], (v, to)))
    parts = [outbox[b]]
    for j in range(1, n_b):
        source = (b - j + n_b) % n_b
        pltpu.make_async_copy(outbox.at[0], inbox.at[source], t_recv.at[source]).wait()
        parts.append(inbox[source])
    candidates, top, total = combine(parts, group)
    midbox[:group, :] = candidates
    midbox[group : group + 1, :] = top
    midbox[group + 1 : group + 2, :] = total
    midbox[group + 2 :, :] = jnp.zeros((STAT_ROWS - 2, LANES), jnp.float32)
    for j in range(1, n_v):
        to = (v + j) % n_v
        sent.append(send(midbox, lastbox.at[v], u_send.at[j], u_recv.at[v], (to, b)))
    lastbox[v] = midbox[...]
    for j in range(1, n_v):
        source = (v - j + n_v) % n_v
        pltpu.make_async_copy(midbox, lastbox.at[source], u_recv.at[source]).wait()
    candidates, top, total = combine([lastbox[s] for s in range(n_v)], group)

    log_norm = top + jnp.log(jnp.where(total > 0.0, total, 1.0))
    cutoff = row_to_column(keep_ref[...].astype(jnp.float32), b * group, group)
    kept = iota((group, LANES), 1).astype(jnp.float32) < cutoff
    kept_top = jnp.max(jnp.where(kept, candidates, -3e38), axis=1, keepdims=True)
    shifted = jnp.where(kept, candidates - kept_top, 0.0)
    kept_exp = jnp.where(kept, jnp.exp(shifted), 0.0)
    kept_sum = jnp.sum(kept_exp, axis=1, keepdims=True)
    kept_log = column_to_row(kept_top + jnp.log(kept_sum))
    norm_ref[...] = log_norm[:, :group]
    mass_ref[...] = (kept_log - log_norm)[:, :group]
    renorm_ref[...] = kept_exp / kept_sum
    for copy in sent:
        copy.wait_send()


def solution(mesh):
    n_v, n_b = mesh.shape["vocab"], mesh.shape["batch"]

    def local(rows, gain, w, heat, choice, ids, keep):
        group, fpd = rows.shape
        depth, cols = w.shape
        slots = n_b * group
        kc = min(fpd, CHUNK_ROWS)
        n_slots = min(depth // kc, max(1, STREAM_BYTES // (kc * cols * 2)))
        box = group + STAT_ROWS
        vmem = pl.BlockSpec(memory_space=pltpu.VMEM)
        log_norm, mass, renormed = pl.pallas_call(
            functools.partial(kernel, n_v, n_b, n_slots, kc),
            out_shape=(
                jax.ShapeDtypeStruct((1, group), jnp.float32),
                jax.ShapeDtypeStruct((1, group), jnp.float32),
                jax.ShapeDtypeStruct((group, ids.shape[1]), jnp.float32),
            ),
            in_specs=[vmem, vmem, pl.BlockSpec(memory_space=pl.ANY), vmem, vmem, vmem, vmem],
            out_specs=(vmem, vmem, vmem),
            scratch_shapes=[
                pltpu.VMEM((n_slots, kc, cols), jnp.bfloat16),
                pltpu.VMEM((n_b, n_v, group, fpd), jnp.bfloat16),
                pltpu.VMEM((depth // kc, slots, kc), jnp.bfloat16),
                pltpu.VMEM((slots, cols), jnp.float32),
                pltpu.VMEM((n_b, box, LANES), jnp.float32),
                pltpu.VMEM((n_b, box, LANES), jnp.float32),
                pltpu.VMEM((box, LANES), jnp.float32),
                pltpu.VMEM((n_v, box, LANES), jnp.float32),
                pltpu.SemaphoreType.DMA((n_slots,)),
                pltpu.SemaphoreType.DMA((n_b, n_v)),
                pltpu.SemaphoreType.DMA((n_v,)),
                pltpu.SemaphoreType.DMA((n_b // 2, n_v)),
                pltpu.SemaphoreType.DMA((n_b // 2, n_v)),
                pltpu.SemaphoreType.DMA((n_b,)),
                pltpu.SemaphoreType.DMA((n_b,)),
                pltpu.SemaphoreType.DMA((n_v,)),
                pltpu.SemaphoreType.DMA((n_v,)),
            ],
            compiler_params=pltpu.CompilerParams(
                collective_id=0,
                has_side_effects=True,
                vmem_limit_bytes=60 * 1024 * 1024,
            ),
        )(
            rows,
            gain.astype(jnp.float32).reshape(n_v, fpd),
            w,
            heat.reshape(1, -1),
            choice.reshape(1, -1),
            ids,
            keep.reshape(1, -1),
        )
        return log_norm.reshape(group), mass.reshape(group), renormed

    placed = (P("batch", "vocab"), P(), P(None, ("vocab", "batch")), P(), P(), P(), P())
    return jax.shard_map(
        local,
        mesh=mesh,
        in_specs=placed,
        out_specs=(P("batch"), P("batch"), P("batch", None)),
        check_vma=False,
    )
```

profile of v0, /device:TPU:0, one launch (start us, length us, event | category | flops | bytes accessed | tf_op | source)
XLA Modules:
  0.0 48.1 jit_solution(5117862312247617412)
XLA Ops:
  0.6 1.3 %reshape.34.gain_ref = f32[8,1024]{1,0:T(8,128)} reshape(bf16[8192]{0:T(1024)(128)(2,1)} %param.8) | data formatting | bytes 49152 | tf_op jit(solution)/shard_map/reshape | solution.py:305
  2.0 42.5 %shard_map.94 = (f32[1,16]{1,0:T(1,128)}, f32[1,16]{1,0:T(1,128)}, f32[16,128]{1,0:T(8,128)}) custom-call(bf16[16,1024]{1,0:T(8,128)(2,1)} %x_ref.1, f32[8,1024]{1,0:T(8,128)} %reshape.34.gain_ref, bf16[8192,4096]{1,0:T(8,128)(2,1)} %w_ref.1, f32[1,16]{1,0:T(1,128)} %bitcast.5, s32[1,64]{1,0:T(1,128)} %bitcast.6, s32[64,128]{1,0:T(8,128)} %ids_ref.1, ...), custom_call_target="tpu_custom_call" | custom-call | tf_op jit(solution)/shard_map/pallas_call | solution.py:270
  44.5 1.1 %copy.13 = f32[16]{0:T(128)} copy(f32[16]{0:T(128)} %bitcast.9) | data formatting | bytes 128
  45.6 1.1 %copy.14 = f32[16]{0:T(128)} copy(f32[16]{0:T(128)} %bitcast.8) | data formatting | bytes 128
  46.8 1.3 %copy.15 = f32[16,128]{1,0:T(8,128)} copy(f32[16,128]{1,0:T(8,128)} %get-tuple-element.14) | data formatting | bytes 16384
where the time goes:
time: 48.4 us; the launch traced here: 48.1 us
  Pallas kernels  42.5 us (88%)
  local copies, waits for them, and re-layouts  4.91 us (10%)
  between operations  0.64 us (1%)
    pallas_call x1, Pallas kernels, local(): pl.pallas_call(functools.partial(kernel, n_v, n_b, n_slots, kc), out_shap...  42.5 us
    unnamed x3, local copies, waits for them, and re-layouts  3.56 us
    reshape x1, local copies, waits for them, and re-layouts, local(): gain.astype(jnp.float32).reshape(n_v, fpd)  1.35 us

commit v1 on v0

v1 whole, which is shorter than its diff:
```python
import functools

import jax
import jax.numpy as jnp
from jax import lax
from jax.experimental import pallas as pl
from jax.experimental.pallas import tpu as pltpu
from jax.sharding import PartitionSpec as P

MESH = pl.DeviceIdType.MESH
epsilon = 1e-06
LANES = 128
TILE = 256
STAT_ROWS = 8
BLOCK_COLS = 512
STREAM_BYTES = 48 * 1024 * 1024
LAST_ROWS = 512
LOW = -3e38


def iota(shape, axis):
    return lax.broadcasted_iota(jnp.int32, shape, axis)


def column_to_row(column):
    rows = column.shape[0]
    diagonal = iota((rows, LANES), 0) == iota((rows, LANES), 1)
    return jnp.sum(jnp.where(diagonal, column, 0.0), axis=0, keepdims=True)


def row_to_column(row, first, rows):
    width = row.shape[1]
    diagonal = iota((rows, width), 0) + first == iota((rows, width), 1)
    return jnp.sum(jnp.where(diagonal, row, 0.0), axis=1, keepdims=True)


def combine(parts, group):
    candidates = parts[0][:group, :]
    top = parts[0][group : group + 1, :]
    for part in parts[1:]:
        candidates = candidates + part[:group, :]
        top = jnp.maximum(top, part[group : group + 1, :])
    total = jnp.zeros_like(top)
    for part in parts:
        total = total + part[group + 1 : group + 2, :] * jnp.exp(
            part[group : group + 1, :] - top
        )
    return candidates, top, total


def flip(value, j):
    out = value
    bit = 1
    while bit <= j:
        if j & bit:
            out = out + bit * (1 - 2 * ((value // bit) % 2))
        bit *= 2
    return out


def kernel(n_v, n_b, n_early, specs, *refs):
    pl.run_scoped(lambda *accs: program(n_v, n_b, n_early, accs, *refs), *specs)


def program(
    n_v,
    n_b,
    n_early,
    accs,
    x_hbm,
    gain_hbm,
    w_hbm,
    heat_hbm,
    choice_hbm,
    ids_hbm,
    keep_hbm,
    out_ref,
    wbuf,
    xbuf,
    lhs,
    gain_in,
    gain_row,
    heat_ref,
    choice_ref,
    ids_ref,
    keep_ref,
    z_stat,
    p_stat,
    stat_out,
    outbox,
    inbox,
    midbox,
    lastbox,
    w_sem,
    l_sem,
    in_sem,
    x_recv,
    x_send,
    z_recv,
    z_send,
    p_recv,
    p_send,
    t_recv,
    t_send,
    u_recv,
    u_send,
):
    v = lax.axis_index("vocab")
    b = lax.axis_index("batch")
    side = n_b // 2
    n_z = n_v // side
    z = v // side
    y = v % side
    x = b // 2
    c = b % 2
    n_p = 2 * side * side
    group, fpd = x_hbm.shape
    slots = n_b * group
    depth, cols = w_hbm.shape
    n_slots, kz, bc = wbuf.shape
    n_blocks = cols // bc
    halves = bc // TILE
    n_last = max(1, kz // LAST_ROWS)

    def device(x_, y_, z_, c_):
        return (z_ * side + y_, 2 * x_ + c_)

    def place(x_, y_, c_):
        return (x_ * side + y_) * 2 + c_

    mine = place(x, y, c)

    plane = []
    for dx in range(side):
        for dy in range(side):
            for dc in range(2):
                if dx + dy + dc > 0:
                    plane.append(((x + dx) % side, (y + dy) % side, (c + dc) % 2))
    order = [flip(z, j) for j in range(n_z)]

    loads = [
        pltpu.make_async_copy(src, dst, in_sem.at[i])
        for i, (src, dst) in enumerate(
            [
                (x_hbm, xbuf.at[v, b]),
                (gain_hbm, gain_in),
                (heat_hbm, heat_ref),
                (choice_hbm, choice_ref),
                (ids_hbm, ids_ref),
                (keep_hbm, keep_ref),
            ]
        )
    ]
    for copy in loads:
        copy.start()

    tasks = [(j, n) for j in range(n_z) for n in range(n_early)]
    tasks += [(j, n) for n in range(n_early, n_blocks) for j in range(n_z)]
    n_tasks = len(tasks)

    def stream(t):
        j, n = tasks[t]
        slot = t % n_slots
        row = pl.multiple_of(order[j] * kz, kz)
        columns = pl.ds(n * bc, bc)
        if t < n_tasks - 1:
            return [
                pltpu.make_async_copy(
                    w_hbm.at[pl.ds(row, kz), columns], wbuf.at[slot], w_sem.at[slot]
                )
            ]
        piece = kz // n_last
        return [
            pltpu.make_async_copy(
                w_hbm.at[pl.ds(row + i * piece, piece), columns],
                wbuf.at[slot, pl.ds(i * piece, piece)],
                l_sem.at[i],
            )
            for i in range(n_last)
        ]

    for t in range(min(n_slots, n_tasks)):
        for copy in stream(t):
            copy.start()

    barrier = pltpu.get_barrier_semaphore()
    for j in range(1, n_z):
        pl.semaphore_signal(
            barrier, inc=1, device_id=device(x, y, order[j], c), device_id_type=MESH
        )
    for px, py, pc in plane:
        pl.semaphore_signal(
            barrier, inc=1, device_id=device(px, py, z, pc), device_id_type=MESH
        )

    loads[0].wait()
    own = xbuf[v, b].astype(jnp.float32)
    own = own * own
    partial = own[:, :LANES]
    for t in range(1, fpd // LANES):
        partial = partial + own[:, t * LANES : (t + 1) * LANES]
    partial = column_to_row(jnp.sum(partial, axis=1, keepdims=True))
    stat_out[0] = partial
    z_stat[z] = partial

    pl.semaphore_wait(barrier, n_z - 1 + n_p - 1)

    sent = []

    def send(src, dst, send_sem, recv_sem, to):
        copy = pltpu.make_async_remote_copy(
            src_ref=src,
            dst_ref=dst,
            send_sem=send_sem,
            recv_sem=recv_sem,
            device_id=to,
            device_id_type=MESH,
        )
        copy.start()
        sent.append(copy)

    counter = [0]

    def forward(v_, b_, to):
        block = xbuf.at[v_, b_]
        send(block, block, x_send.at[counter[0]], x_recv.at[v_, b_], to)
        counter[0] += 1

    def arrived(v_, b_):
        pltpu.make_async_copy(x_hbm, xbuf.at[v_, b_], x_recv.at[v_, b_]).wait()

    def peers(i, first):
        a = 1 - c if first else c
        return (x + i * a) % side, (y + i * (1 - a)) % side

    def sources(i, first):
        a = 1 - c if first else c
        return (x + (side - i) * a) % side, (y + (side - i) * (1 - a)) % side

    for j in range(1, n_z):
        send(
            stat_out.at[0],
            z_stat.at[z],
            z_send.at[j],
            z_recv.at[z],
            device(x, y, order[j], c),
        )
    for j in reversed(range(1, n_z)):
        forward(v, b, device(x, y, order[j], c))

    def spread(v_, b_, first):
        if first:
            for i in range(1, side):
                px, py = peers(i, True)
                forward(v_, b_, device(px, py, z, c))
        for i in range(1, side):
            px, py = peers(i, False)
            forward(v_, b_, device(px, py, z, c))
        forward(v_, b_, device(x, y, z, 1 - c))

    def step_z(j):
        v_ = order[j] * side + y
        if j > 0:
            arrived(v_, b)
        spread(v_, b, True)

    def step_f(j):
        for i in range(1, side):
            fx, fy = sources(i, True)
            v_, b_ = order[j] * side + fy, 2 * fx + c
            arrived(v_, b_)
            spread(v_, b_, False)

    def step_s(j):
        for i in range(1, side):
            sx, sy = sources(i, False)
            v_, b_ = order[j] * side + sy, 2 * sx + c
            arrived(v_, b_)
            forward(v_, b_, device(x, y, z, 1 - c))

    def step_d(j):
        for i in range(1, side):
            for k in range(1, side):
                fx, fy = sources(i, True)
                sx, sy = sources(k, False)
                dx = (fx + sx - x + side) % side
                dy = (fy + sy - y + side) % side
                v_, b_ = order[j] * side + dy, 2 * dx + c
                arrived(v_, b_)
                forward(v_, b_, device(x, y, z, 1 - c))

    def stat_z():
        for j in range(1, n_z):
            source = order[j]
            pltpu.make_async_copy(
                stat_out.at[0], z_stat.at[source], z_recv.at[source]
            ).wait()
        total = z_stat[0]
        for j in range(1, n_z):
            total = total + z_stat[j]
        stat_out[1] = total
        p_stat[mine] = total
        for i, (px, py, pc) in enumerate(plane):
            send(
                stat_out.at[1],
                p_stat.at[mine],
                p_send.at[i],
                p_recv.at[mine],
                device(px, py, z, pc),
            )

    def stat_p():
        for px, py, pc in plane:
            source = place(px, py, pc)
            pltpu.make_async_copy(
                stat_out.at[1], p_stat.at[source], p_recv.at[source]
            ).wait()
        columns = []
        for bx in range(side):
            for bcore in range(2):
                total = p_stat[place(bx, 0, bcore)]
                for by in range(1, side):
                    total = total + p_stat[place(bx, by, bcore)]
                columns.append(row_to_column(total, 0, group))
        mean_square = jnp.concatenate(columns, axis=0) / depth
        return lax.rsqrt(mean_square + epsilon)

    step_z(0)
    done = {"z": 1, "f": 0, "s": 0, "d": 0}

    def advance(kind):
        if done[kind] < n_z:
            {"z": step_z, "f": step_f, "s": step_s, "d": step_d}[kind](done[kind])
            done[kind] += 1

    for copy in loads[1:]:
        copy.wait()
    gain_row[...] = gain_in[...].astype(jnp.float32)

    advance("f")
    advance("z")
    advance("s")
    advance("f")
    advance("z")
    advance("d")
    advance("s")
    stat_z()
    advance("f")
    advance("z")
    advance("d")
    advance("s")
    while done["z"] < n_z:
        advance("f")
        advance("z")
        advance("d")
        advance("s")
    factor = stat_p()

    choice = row_to_column(choice_ref[...].astype(jnp.float32), 0, slots)
    n_heat = heat_ref.shape[1]
    member = choice == iota((slots, n_heat), 1).astype(jnp.float32)
    heat = jnp.sum(jnp.where(member, heat_ref[...], 0.0), axis=1, keepdims=True)
    cool = 1.0 / heat

    local_ids = ids_ref[...] - (v * n_b + b) * cols
    tile_of = local_ids >> 7
    lane_of = local_ids & (LANES - 1)

    def normalise(j):
        for k in range(side):
            at = order[j] * side + k
            values = xbuf[at].reshape(slots, fpd).astype(jnp.float32)
            for t in range(fpd // LANES):
                lanes = slice(t * LANES, (t + 1) * LANES)
                gain = gain_row[pl.ds(at * (fpd // LANES) + t, 1), :]
                lhs[j, :, k * fpd + t * LANES : k * fpd + (t + 1) * LANES] = (
                    values[:, lanes] * factor * gain
                ).astype(jnp.bfloat16)

    def partner_blocks(j):
        for k in range(side):
            for bx in range(side):
                arrived(order[j] * side + k, 2 * bx + 1 - c)

    n_acc = len(accs) // halves
    for acc in accs:
        pltpu.matmul_pop(acc)
    state = [
        jnp.full((slots, LANES), LOW, jnp.float32),
        jnp.zeros((slots, LANES), jnp.float32),
        jnp.zeros((slots, LANES), jnp.float32),
    ]

    def run(t):
        j, n = tasks[t]
        slot = t % n_slots
        pieces = stream(t)
        rows = kz // len(pieces)
        at = (n % n_acc) * halves
        turn = 0
        for i, piece in enumerate(pieces):
            piece.wait()
            for k in range(rows // TILE):
                r = i * rows + k * TILE
                for q in range(halves):
                    pltpu.matmul_push_rhs(
                        wbuf[slot, r : r + TILE, q * TILE : (q + 1) * TILE],
                        staging_register=turn % 2,
                        mxu_index=q,
                    )
                    pltpu.matmul_acc_lhs(
                        accs[at + q],
                        lhs[j, :, r : r + TILE],
                        load_staged_rhs=turn % 2,
                    )
                turn += 1
        if t + n_slots < n_tasks:
            for copy in stream(t + n_slots):
                copy.start()

    def finish(n):
        top, total, picked = state
        at = (n % n_acc) * halves
        parts = []
        for q in range(halves):
            scores = pltpu.matmul_pop(accs[at + q]) * cool
            for h in range(TILE // LANES):
                parts.append(scores[:, h * LANES : (h + 1) * LANES])
        new_top = top
        for i, part in enumerate(parts):
            new_top = jnp.maximum(new_top, part)
            found = jnp.take_along_axis(
                part, lane_of, axis=1, mode="promise_in_bounds"
            )
            picked = jnp.where(tile_of == n * (bc // LANES) + i, found, picked)
        total = total * jnp.exp(top - new_top)
        for part in parts:
            total = total + jnp.exp(part - new_top)
        state[:] = [new_top, total, picked]

    pending = []
    t = 0
    for j in range(n_z):
        while done["d"] <= j:
            advance("f")
            advance("s")
            advance("d")
        partner_blocks(j)
        normalise(j)
        for n in range(n_early):
            run(t)
            t += 1
    pending = list(range(n_early))
    for n in range(n_early, n_blocks):
        while pending and (len(pending) >= n_acc or pending[0] % n_acc == n % n_acc):
            finish(pending.pop(0))
        for j in range(n_z):
            run(t)
            t += 1
            if pending:
                finish(pending.pop(0))
        pending.append(n)
    while pending:
        finish(pending.pop(0))

    top, total, picked = state
    peak = jnp.max(top, axis=1, keepdims=True)
    total = jnp.sum(total * jnp.exp(top - peak), axis=1, keepdims=True)
    for p in range(n_b):
        rows = slice(p * group, (p + 1) * group)
        outbox[p, :group, :] = picked[rows, :]
        outbox[p, group : group + 1, :] = column_to_row(peak[rows, :])
        outbox[p, group + 1 : group + 2, :] = column_to_row(total[rows, :])
        outbox[p, group + 2 :, :] = jnp.zeros((STAT_ROWS - 2, LANES), jnp.float32)

    for i, (px, py, pc) in enumerate(plane):
        send(
            outbox.at[2 * px + pc],
            inbox.at[mine],
            t_send.at[i],
            t_recv.at[mine],
            device(px, py, z, pc),
        )
    inbox[mine] = outbox[b]
    for px, py, pc in plane:
        source = place(px, py, pc)
        pltpu.make_async_copy(outbox.at[0], inbox.at[source], t_recv.at[source]).wait()
    candidates, top, total = combine([inbox[s] for s in range(n_p)], group)
    midbox[:group, :] = candidates
    midbox[group : group + 1, :] = top
    midbox[group + 1 : group + 2, :] = total
    midbox[group + 2 :, :] = jnp.zeros((STAT_ROWS - 2, LANES), jnp.float32)
    for j in range(1, n_z):
        send(midbox, lastbox.at[z], u_send.at[j], u_recv.at[z], device(x, y, order[j], c))
    lastbox[z] = midbox[...]
    for j in range(1, n_z):
        source = order[j]
        pltpu.make_async_copy(midbox, lastbox.at[source], u_recv.at[source]).wait()
    candidates, top, total = combine([lastbox[s] for s in range(n_z)], group)

    log_norm = top + jnp.log(jnp.where(total > 0.0, total, 1.0))
    cutoff = row_to_column(keep_ref[...].astype(jnp.float32), b * group, group)
    kept = iota((group, LANES), 1).astype(jnp.float32) < cutoff
    kept_top = jnp.max(jnp.where(kept, candidates, LOW), axis=1, keepdims=True)
    shifted = jnp.where(kept, candidates - kept_top, 0.0)
    kept_exp = jnp.where(kept, jnp.exp(shifted), 0.0)
    kept_sum = jnp.sum(kept_exp, axis=1, keepdims=True)
    kept_log = column_to_row(kept_top + jnp.log(kept_sum))
    out_ref[:group, :] = kept_exp / kept_sum
    out_ref[group : group + 1, :] = log_norm
    out_ref[group + 1 : group + 2, :] = kept_log - log_norm
    out_ref[group + 2 :, :] = jnp.zeros((STAT_ROWS - 2, LANES), jnp.float32)
    for copy in sent:
        copy.wait_send()


def split(all_ref, norm_ref, mass_ref, renorm_ref):
    group = renorm_ref.shape[0]
    renorm_ref[...] = all_ref[:group, :]
    norm_ref[...] = all_ref[group : group + 1, :group]
    mass_ref[...] = all_ref[group + 1 : group + 2, :group]


def solution(mesh):
    n_v, n_b = mesh.shape["vocab"], mesh.shape["batch"]

    def local(rows, gain, w, heat, choice, ids, keep):
        group, fpd = rows.shape
        depth, cols = w.shape
        slots = n_b * group
        side = n_b // 2
        n_z = n_v // side
        n_p = 2 * side * side
        kz = depth // n_z
        bc = min(cols, BLOCK_COLS)
        n_blocks = cols // bc
        n_early = max(1, n_blocks // 2)
        n_slots = min(n_z * n_blocks, max(2, STREAM_BYTES // (kz * bc * 2)))
        box = group + STAT_ROWS
        hops = side - 1
        n_sends = n_z - 1 + n_z * (4 * hops + 2 * hops * hops + 1)
        n_acc = max(n_early, min(2, n_blocks))
        accs = [
            pltpu.ACC(q)((slots, TILE), jnp.float32)
            for _ in range(n_acc)
            for q in range(bc // TILE)
        ]
        vmem = pl.BlockSpec(memory_space=pltpu.VMEM)
        anywhere = pl.BlockSpec(memory_space=pl.ANY)
        gain_rows = gain.reshape(depth // LANES, LANES)
        packed = pl.pallas_call(
            functools.partial(kernel, n_v, n_b, n_early, accs),
            out_shape=jax.ShapeDtypeStruct((box, LANES), jnp.float32),
            in_specs=[anywhere] * 7,
            out_specs=vmem,
            scratch_shapes=[
                pltpu.VMEM((n_slots, kz, bc), jnp.bfloat16),
                pltpu.VMEM((n_v, n_b, group, fpd), jnp.bfloat16),
                pltpu.VMEM((n_z, slots, kz), jnp.bfloat16),
                pltpu.VMEM(gain_rows.shape, jnp.bfloat16),
                pltpu.VMEM(gain_rows.shape, jnp.float32),
                pltpu.VMEM((1, heat.shape[0]), jnp.float32),
                pltpu.VMEM((1, slots), jnp.int32),
                pltpu.VMEM(ids.shape, jnp.int32),
                pltpu.VMEM((1, slots), jnp.int32),
                pltpu.VMEM((n_z, 1, LANES), jnp.float32),
                pltpu.VMEM((n_p, 1, LANES), jnp.float32),
                pltpu.VMEM((2, 1, LANES), jnp.float32),
                pltpu.VMEM((n_b, box, LANES), jnp.float32),
                pltpu.VMEM((n_p, box, LANES), jnp.float32),
                pltpu.VMEM((box, LANES), jnp.float32),
                pltpu.VMEM((n_z, box, LANES), jnp.float32),
                pltpu.SemaphoreType.DMA((n_slots,)),
                pltpu.SemaphoreType.DMA((max(1, kz // LAST_ROWS),)),
                pltpu.SemaphoreType.DMA((6,)),
                pltpu.SemaphoreType.DMA((n_v, n_b)),
                pltpu.SemaphoreType.DMA((n_sends,)),
                pltpu.SemaphoreType.DMA((n_z,)),
                pltpu.SemaphoreType.DMA((n_z,)),
                pltpu.SemaphoreType.DMA((n_p,)),
                pltpu.SemaphoreType.DMA((n_p,)),
                pltpu.SemaphoreType.DMA((n_p,)),
                pltpu.SemaphoreType.DMA((n_p,)),
                pltpu.SemaphoreType.DMA((n_z,)),
                pltpu.SemaphoreType.DMA((n_z,)),
            ],
            compiler_params=pltpu.CompilerParams(
                collective_id=0,
                has_side_effects=True,
                vmem_limit_bytes=60 * 1024 * 1024,
            ),
        )(
            rows,
            gain_rows,
            w,
            heat.reshape(1, -1),
            choice.reshape(1, -1),
            ids,
            keep.reshape(1, -1),
        )
        log_norm, mass, renormed = pl.pallas_call(
            split,
            out_shape=(
                jax.ShapeDtypeStruct((1, group), jnp.float32),
                jax.ShapeDtypeStruct((1, group), jnp.float32),
                jax.ShapeDtypeStruct((group, ids.shape[1]), jnp.float32),
            ),
            in_specs=[vmem],
            out_specs=(vmem, vmem, vmem),
        )(packed)
        return log_norm.reshape(group), mass.reshape(group), renormed

    placed = (P("batch", "vocab"), P(), P(None, ("vocab", "batch")), P(), P(), P(), P())
    return jax.shard_map(
        local,
        mesh=mesh,
        in_specs=placed,
        out_specs=(P("batch"), P("batch"), P("batch", None)),
        check_vma=False,
    )
```

time: 48.4 us -> 52.6 us (1.087)
  Pallas kernels: 42.5 us -> 51.7 us
  local copies, waits for them, and re-layouts: 4.91 us -> 0 us
    pallas_call x1 -> x2, Pallas kernels: 42.5 us -> 51.7 us  [the longest x1 50.4 us: local(): pl.pallas_call(functools.partial(kernel, n_v, n_b, n_early, accs), out_sh...]
    unnamed x3 -> x0, local copies, waits for them, and re-layouts: 3.56 us -> none
    reshape x1 -> x0, local copies, waits for them, and re-layouts: 1.35 us -> none  [local(): gain.astype(jnp.float32).reshape(n_v, fpd)]
where the time goes in v1:
time: 52.6 us; the launch traced here: 52.4 us
  Pallas kernels  51.7 us (98%)
  between operations  0.64 us (1%)
    pallas_call x1, Pallas kernels, local(): pl.pallas_call(functools.partial(kernel, n_v, n_b, n_early, accs), out_sh...  50.4 us
    pallas_call x1, Pallas kernels, local(): pl.pallas_call(split, out_shape=(jax.ShapeDtypeStruct((1, group), jnp.flo...  1.32 us

profile of v1, /device:TPU:0, one launch (start us, length us, event | category | flops | bytes accessed | tf_op | source)
XLA Modules:
  0.0 52.4 jit_solution(2781736398000094936)
XLA Ops:
  0.6 50.4 %shard_map.94.all_ref = f32[24,128]{1,0:T(8,128)} custom-call(bf16[16,1024]{1,0:T(8,128)(2,1)} %refs_0_.1, bf16[64,128]{1,0:T(8,128)(2,1)} %bitcast.6, bf16[8192,4096]{1,0:T(8,128)(2,1)} %refs_2_.1, f32[1,16]{1,0:T(1,128)} %bitcast.7, s32[1,64]{1,0:T(1,128)} %bitcast.8, s32[64,128]{1,0:T(8,128)} %refs_5_.1, s32[1,64]{1,0:T(1,128)} %bitcast.9), custom_call_target="tpu_custom_call" | custom-call | tf_op jit(solution)/shard_map/pallas_call | solution.py:551
  51.1 1.3 %shard_map.95 = (f32[1,16]{1,0:T(1,128)}, f32[1,16]{1,0:T(1,128)}, f32[16,128]{1,0:T(8,128)}) custom-call(f32[24,128]{1,0:T(8,128)} %shard_map.94.all_ref), custom_call_target="tpu_custom_call" | custom-call | tf_op jit(solution)/shard_map/pallas_call | solution.py:601

commit v2 on v1

--- a/solution.py
+++ b/solution.py
@@ -11,7 +11,7 @@
 epsilon = 1e-06
 LANES = 128
 TILE = 256
-STAT_ROWS = 8
+STAT_ROWS = 2
 BLOCK_COLS = 512
 STREAM_BYTES = 48 * 1024 * 1024
 LAST_ROWS = 512
@@ -181,7 +181,7 @@
 
     for t in range(min(n_slots, n_tasks)):
         for copy in stream(t):
-            copy.start()
+            copy.start(priority=1)
 
     barrier = pltpu.get_barrier_semaphore()
     for j in range(1, n_z):
@@ -229,13 +229,8 @@
     def arrived(v_, b_):
         pltpu.make_async_copy(x_hbm, xbuf.at[v_, b_], x_recv.at[v_, b_]).wait()
 
-    def peers(i, first):
-        a = 1 - c if first else c
-        return (x + i * a) % side, (y + i * (1 - a)) % side
-
-    def sources(i, first):
-        a = 1 - c if first else c
-        return (x + (side - i) * a) % side, (y + (side - i) * (1 - a)) % side
+    same = [(dx, dy) for dx in range(side) for dy in range(side) if dx + dy > 0]
+    same.sort(key=lambda d: -d[0] - d[1])
 
     for j in range(1, n_z):
         send(
@@ -248,46 +243,20 @@
     for j in reversed(range(1, n_z)):
         forward(v, b, device(x, y, order[j], c))
 
-    def spread(v_, b_, first):
-        if first:
-            for i in range(1, side):
-                px, py = peers(i, True)
-                forward(v_, b_, device(px, py, z, c))
-        for i in range(1, side):
-            px, py = peers(i, False)
-            forward(v_, b_, device(px, py, z, c))
-        forward(v_, b_, device(x, y, z, 1 - c))
-
     def step_z(j):
         v_ = order[j] * side + y
         if j > 0:
             arrived(v_, b)
-        spread(v_, b, True)
-
-    def step_f(j):
-        for i in range(1, side):
-            fx, fy = sources(i, True)
-            v_, b_ = order[j] * side + fy, 2 * fx + c
-            arrived(v_, b_)
-            spread(v_, b_, False)
-
-    def step_s(j):
-        for i in range(1, side):
-            sx, sy = sources(i, False)
-            v_, b_ = order[j] * side + sy, 2 * sx + c
+        for dx, dy in same:
+            forward(v_, b, device((x + dx) % side, (y + dy) % side, z, c))
+        forward(v_, b, device(x, y, z, 1 - c))
+
+    def step_p(j):
+        for dx, dy in reversed(same):
+            px, py = (x - dx + side) % side, (y - dy + side) % side
+            v_, b_ = order[j] * side + py, 2 * px + c
             arrived(v_, b_)
             forward(v_, b_, device(x, y, z, 1 - c))
-
-    def step_d(j):
-        for i in range(1, side):
-            for k in range(1, side):
-                fx, fy = sources(i, True)
-                sx, sy = sources(k, False)
-                dx = (fx + sx - x + side) % side
-                dy = (fy + sy - y + side) % side
-                v_, b_ = order[j] * side + dy, 2 * dx + c
-                arrived(v_, b_)
-                forward(v_, b_, device(x, y, z, 1 - c))
 
     def stat_z():
         for j in range(1, n_z):
@@ -326,34 +295,19 @@
         return lax.rsqrt(mean_square + epsilon)
 
     step_z(0)
-    done = {"z": 1, "f": 0, "s": 0, "d": 0}
-
-    def advance(kind):
-        if done[kind] < n_z:
-            {"z": step_z, "f": step_f, "s": step_s, "d": step_d}[kind](done[kind])
-            done[kind] += 1
-
     for copy in loads[1:]:
         copy.wait()
     gain_row[...] = gain_in[...].astype(jnp.float32)
-
-    advance("f")
-    advance("z")
-    advance("s")
-    advance("f")
-    advance("z")
-    advance("d")
-    advance("s")
+    early = max(1, n_z // 2)
+    for j in range(1, early):
+        step_z(j)
+    step_p(0)
+    for j in range(early, n_z - 1):
+        step_z(j)
     stat_z()
-    advance("f")
-    advance("z")
-    advance("d")
-    advance("s")
-    while done["z"] < n_z:
-        advance("f")
-        advance("z")
-        advance("d")
-        advance("s")
+    step_z(n_z - 1)
+    for j in range(1, early):
+        step_p(j)
     factor = stat_p()
 
     choice = row_to_column(choice_ref[...].astype(jnp.float32), 0, slots)
@@ -416,7 +370,7 @@
                 turn += 1
         if t + n_slots < n_tasks:
             for copy in stream(t + n_slots):
-                copy.start()
+                copy.start(priority=1)
 
     def finish(n):
         top, total, picked = state
@@ -441,11 +395,9 @@
     pending = []
     t = 0
     for j in range(n_z):
-        while done["d"] <= j:
-            advance("f")
-            advance("s")
-            advance("d")
         partner_blocks(j)
+        if early <= j + early - 1 < n_z and j > 0:
+            step_p(j + early - 1)
         normalise(j)
         for n in range(n_early):
             run(t)
@@ -471,7 +423,6 @@
         outbox[p, :group, :] = picked[rows, :]
         outbox[p, group : group + 1, :] = column_to_row(peak[rows, :])
         outbox[p, group + 1 : group + 2, :] = column_to_row(total[rows, :])
-        outbox[p, group + 2 :, :] = jnp.zeros((STAT_ROWS - 2, LANES), jnp.float32)
 
     for i, (px, py, pc) in enumerate(plane):
         send(
@@ -489,7 +440,6 @@
     midbox[:group, :] = candidates
     midbox[group : group + 1, :] = top
     midbox[group + 1 : group + 2, :] = total
-    midbox[group + 2 :, :] = jnp.zeros((STAT_ROWS - 2, LANES), jnp.float32)
     for j in range(1, n_z):
         send(midbox, lastbox.at[z], u_send.at[j], u_recv.at[z], device(x, y, order[j], c))
     lastbox[z] = midbox[...]
@@ -509,7 +459,6 @@
     out_ref[:group, :] = kept_exp / kept_sum
     out_ref[group : group + 1, :] = log_norm
     out_ref[group + 1 : group + 2, :] = kept_log - log_norm
-    out_ref[group + 2 :, :] = jnp.zeros((STAT_ROWS - 2, LANES), jnp.float32)
     for copy in sent:
         copy.wait_send()
 
@@ -534,12 +483,11 @@
         kz = depth // n_z
         bc = min(cols, BLOCK_COLS)
         n_blocks = cols // bc
-        n_early = max(1, n_blocks // 2)
+        n_early = max(1, n_blocks - n_blocks // 4)
         n_slots = min(n_z * n_blocks, max(2, STREAM_BYTES // (kz * bc * 2)))
         box = group + STAT_ROWS
-        hops = side - 1
-        n_sends = n_z - 1 + n_z * (4 * hops + 2 * hops * hops + 1)
-        n_acc = max(n_early, min(2, n_blocks))
+        n_sends = n_z - 1 + n_z * (2 * side * side - 1)
+        n_acc = max(n_early, min(8, n_blocks))
         accs = [
             pltpu.ACC(q)((slots, TILE), jnp.float32)
             for _ in range(n_acc)

time: 52.6 us -> 38.9 us (0.74)
  Pallas kernels: 51.7 us -> 38 us
    pallas_call x1, Pallas kernels: 50.4 us -> 36.7 us  [local(): pl.pallas_call(functools.partial(kernel, n_v, n_b, n_early, accs), out_sh...]
where the time goes in v2:
time: 38.9 us; the launch traced here: 38.6 us
  Pallas kernels  38 us (98%)
  between operations  0.64 us (2%)
    pallas_call x1, Pallas kernels, local(): pl.pallas_call(functools.partial(kernel, n_v, n_b, n_early, accs), out_sh...  36.7 us
    pallas_call x1, Pallas kernels, local(): pl.pallas_call(split, out_shape=(jax.ShapeDtypeStruct((1, group), jnp.flo...  1.32 us

profile of v2, /device:TPU:0, one launch (start us, length us, event | category | flops | bytes accessed | tf_op | source)
XLA Modules:
  0.0 38.6 jit_solution(1599397463777174360)
XLA Ops:
  0.6 36.7 %shard_map.94.all_ref = f32[18,128]{1,0:T(8,128)} custom-call(bf16[16,1024]{1,0:T(8,128)(2,1)} %refs_0_.1, bf16[64,128]{1,0:T(8,128)(2,1)} %bitcast.6, bf16[8192,4096]{1,0:T(8,128)(2,1)} %refs_2_.1, f32[1,16]{1,0:T(1,128)} %bitcast.7, s32[1,64]{1,0:T(1,128)} %bitcast.8, s32[64,128]{1,0:T(8,128)} %refs_5_.1, s32[1,64]{1,0:T(1,128)} %bitcast.9), custom_call_target="tpu_custom_call" | custom-call | tf_op jit(solution)/shard_map/pallas_call | solution.py:499
  37.3 1.3 %shard_map.95 = (f32[1,16]{1,0:T(1,128)}, f32[1,16]{1,0:T(1,128)}, f32[16,128]{1,0:T(8,128)}) custom-call(f32[18,128]{1,0:T(8,128)} %shard_map.94.all_ref), custom_call_target="tpu_custom_call" | custom-call | tf_op jit(solution)/shard_map/pallas_call | solution.py:549

commit v3 on v2

--- a/solution.py
+++ b/solution.py
@@ -58,14 +58,13 @@
     return out
 
 
-def kernel(n_v, n_b, n_early, specs, *refs):
-    pl.run_scoped(lambda *accs: program(n_v, n_b, n_early, accs, *refs), *specs)
+def kernel(n_v, n_b, specs, *refs):
+    pl.run_scoped(lambda *accs: program(n_v, n_b, accs, *refs), *specs)
 
 
 def program(
     n_v,
     n_b,
-    n_early,
     accs,
     x_hbm,
     gain_hbm,
@@ -138,6 +137,16 @@
                     plane.append(((x + dx) % side, (y + dy) % side, (c + dc) % 2))
     order = [flip(z, j) for j in range(n_z)]
 
+    barrier = pltpu.get_barrier_semaphore()
+    for j in range(1, n_z):
+        pl.semaphore_signal(
+            barrier, inc=1, device_id=device(x, y, order[j], c), device_id_type=MESH
+        )
+    for px, py, pc in plane:
+        pl.semaphore_signal(
+            barrier, inc=1, device_id=device(px, py, z, pc), device_id_type=MESH
+        )
+
     loads = [
         pltpu.make_async_copy(src, dst, in_sem.at[i])
         for i, (src, dst) in enumerate(
@@ -154,8 +163,7 @@
     for copy in loads:
         copy.start()
 
-    tasks = [(j, n) for j in range(n_z) for n in range(n_early)]
-    tasks += [(j, n) for n in range(n_early, n_blocks) for j in range(n_z)]
+    tasks = [(j, n) for j in range(n_z) for n in range(n_blocks)]
     n_tasks = len(tasks)
 
     def stream(t):
@@ -183,16 +191,6 @@
         for copy in stream(t):
             copy.start(priority=1)
 
-    barrier = pltpu.get_barrier_semaphore()
-    for j in range(1, n_z):
-        pl.semaphore_signal(
-            barrier, inc=1, device_id=device(x, y, order[j], c), device_id_type=MESH
-        )
-    for px, py, pc in plane:
-        pl.semaphore_signal(
-            barrier, inc=1, device_id=device(px, py, z, pc), device_id_type=MESH
-        )
-
     loads[0].wait()
     own = xbuf[v, b].astype(jnp.float32)
     own = own * own
@@ -230,7 +228,7 @@
         pltpu.make_async_copy(x_hbm, xbuf.at[v_, b_], x_recv.at[v_, b_]).wait()
 
     same = [(dx, dy) for dx in range(side) for dy in range(side) if dx + dy > 0]
-    same.sort(key=lambda d: -d[0] - d[1])
+    same.sort(key=lambda d: d[1])
 
     for j in range(1, n_z):
         send(
@@ -240,9 +238,6 @@
             z_recv.at[z],
             device(x, y, order[j], c),
         )
-    for j in reversed(range(1, n_z)):
-        forward(v, b, device(x, y, order[j], c))
-
     def step_z(j):
         v_ = order[j] * side + y
         if j > 0:
@@ -251,12 +246,11 @@
             forward(v_, b, device((x + dx) % side, (y + dy) % side, z, c))
         forward(v_, b, device(x, y, z, 1 - c))
 
-    def step_p(j):
-        for dx, dy in reversed(same):
-            px, py = (x - dx + side) % side, (y - dy + side) % side
-            v_, b_ = order[j] * side + py, 2 * px + c
-            arrived(v_, b_)
-            forward(v_, b_, device(x, y, z, 1 - c))
+    def step_p(j, dx, dy):
+        px, py = (x - dx + side) % side, (y - dy + side) % side
+        v_, b_ = order[j] * side + py, 2 * px + c
+        arrived(v_, b_)
+        forward(v_, b_, device(x, y, z, 1 - c))
 
     def stat_z():
         for j in range(1, n_z):
@@ -295,20 +289,32 @@
         return lax.rsqrt(mean_square + epsilon)
 
     step_z(0)
+    for j in range(1, n_z):
+        forward(v, b, device(x, y, order[j], c))
+
     for copy in loads[1:]:
         copy.wait()
     gain_row[...] = gain_in[...].astype(jnp.float32)
-    early = max(1, n_z // 2)
-    for j in range(1, early):
-        step_z(j)
-    step_p(0)
-    for j in range(early, n_z - 1):
-        step_z(j)
-    stat_z()
-    step_z(n_z - 1)
-    for j in range(1, early):
-        step_p(j)
-    factor = stat_p()
+    level = [d for d in same if d[1] == 0]
+    rest = [d for d in same if d[1] > 0]
+    relays = [("p", 0, *d) for d in level] + [("z", 1)]
+    relays += [("p", 0, *d) for d in rest]
+    relays += [("z", j) for j in range(2, n_z - 1)] + [("stat",)]
+    relays += [("z", n_z - 1)] if n_z > 2 else []
+    relays += [("p", j, *d) for j in range(1, n_z) for d in same]
+    steps = {"z": step_z, "p": step_p, "stat": stat_z}
+
+    def relay(limit=n_z):
+        if relays and (relays[0][0] != "p" or relays[0][1] <= limit):
+            kind, *rest = relays.pop(0)
+            steps[kind](*rest)
+
+    def ensure(wanted):
+        while any(wanted(item) for item in relays):
+            relay()
+
+    ensure(lambda item: item[0] == "p" and item[1] == 0 and item[3] == 0)
+    ensure(lambda item: item == ("z", 1))
 
     choice = row_to_column(choice_ref[...].astype(jnp.float32), 0, slots)
     n_heat = heat_ref.shape[1]
@@ -320,23 +326,25 @@
     tile_of = local_ids >> 7
     lane_of = local_ids & (LANES - 1)
 
-    def normalise(j):
-        for k in range(side):
-            at = order[j] * side + k
-            values = xbuf[at].reshape(slots, fpd).astype(jnp.float32)
-            for t in range(fpd // LANES):
-                lanes = slice(t * LANES, (t + 1) * LANES)
-                gain = gain_row[pl.ds(at * (fpd // LANES) + t, 1), :]
-                lhs[j, :, k * fpd + t * LANES : k * fpd + (t + 1) * LANES] = (
-                    values[:, lanes] * factor * gain
-                ).astype(jnp.bfloat16)
-
-    def partner_blocks(j):
-        for k in range(side):
-            for bx in range(side):
-                arrived(order[j] * side + k, 2 * bx + 1 - c)
-
-    n_acc = len(accs) // halves
+    def feature_block(j, k):
+        return order[j] * side + ((y + k) % side if j == 0 else k)
+
+    def normalise(j, k, factor):
+        at = feature_block(j, k)
+        values = xbuf[at].reshape(slots, fpd).astype(jnp.float32)
+        for t in range(fpd // LANES):
+            part = values[:, t * LANES : (t + 1) * LANES]
+            if factor is not None:
+                part = part * factor
+            gain = gain_row[pl.ds(at * (fpd // LANES) + t, 1), :]
+            lhs[j, :, k * fpd + t * LANES : k * fpd + (t + 1) * LANES] = (
+                part * gain
+            ).astype(jnp.bfloat16)
+
+    def partner_blocks(j, k):
+        for bx in range(side):
+            arrived(feature_block(j, k), 2 * bx + 1 - c)
+
     for acc in accs:
         pltpu.matmul_pop(acc)
     state = [
@@ -345,20 +353,32 @@
         jnp.zeros((slots, LANES), jnp.float32),
     ]
 
-    def run(t):
+    def run(t, k=None):
         j, n = tasks[t]
         slot = t % n_slots
         pieces = stream(t)
-        rows = kz // len(pieces)
-        at = (n % n_acc) * halves
+        at = (2 * n + (j > 0)) * halves
+        if k is None:
+            rows = kz // len(pieces)
+            spans = [(piece, i * rows, i * rows) for i, piece in enumerate(pieces)]
+        else:
+            rows = fpd
+            if k == 0:
+                for piece in pieces:
+                    piece.wait()
+            spans = [(None, k * fpd, ((y + k) % side) * fpd)]
         turn = 0
-        for i, piece in enumerate(pieces):
-            piece.wait()
-            for k in range(rows // TILE):
-                r = i * rows + k * TILE
+        for piece, left, row in spans:
+            if piece is not None:
+                piece.wait()
+            for i in range(rows // TILE):
+                r = left + i * TILE
+                w = row + i * TILE
+                if k is not None:
+                    w = pl.multiple_of(w, TILE)
                 for q in range(halves):
                     pltpu.matmul_push_rhs(
-                        wbuf[slot, r : r + TILE, q * TILE : (q + 1) * TILE],
+                        wbuf[slot, pl.ds(w, TILE), q * TILE : (q + 1) * TILE],
                         staging_register=turn % 2,
                         mxu_index=q,
                     )
@@ -368,16 +388,17 @@
                         load_staged_rhs=turn % 2,
                     )
                 turn += 1
-        if t + n_slots < n_tasks:
+        if t + n_slots < n_tasks and k in (None, side - 1):
             for copy in stream(t + n_slots):
                 copy.start(priority=1)
 
     def finish(n):
         top, total, picked = state
-        at = (n % n_acc) * halves
+        at = 2 * n * halves
         parts = []
         for q in range(halves):
-            scores = pltpu.matmul_pop(accs[at + q]) * cool
+            scores = pltpu.matmul_pop(accs[at + q]) * warm
+            scores = scores + pltpu.matmul_pop(accs[at + halves + q]) * cool
             for h in range(TILE // LANES):
                 parts.append(scores[:, h * LANES : (h + 1) * LANES])
         new_top = top
@@ -392,28 +413,30 @@
             total = total + jnp.exp(part - new_top)
         state[:] = [new_top, total, picked]
 
-    pending = []
-    t = 0
-    for j in range(n_z):
-        partner_blocks(j)
-        if early <= j + early - 1 < n_z and j > 0:
-            step_p(j + early - 1)
-        normalise(j)
-        for n in range(n_early):
-            run(t)
-            t += 1
-    pending = list(range(n_early))
-    for n in range(n_early, n_blocks):
-        while pending and (len(pending) >= n_acc or pending[0] % n_acc == n % n_acc):
-            finish(pending.pop(0))
-        for j in range(n_z):
-            run(t)
-            t += 1
-            if pending:
-                finish(pending.pop(0))
-        pending.append(n)
-    while pending:
-        finish(pending.pop(0))
+    for k in range(side):
+        if k > 0:
+            ensure(lambda item: item[0] == "p" and item[1] == 0)
+        partner_blocks(0, k)
+        normalise(0, k, None)
+        for n in range(n_blocks):
+            run(n, k)
+            late = k == side - 1 and n >= n_blocks - len(same)
+            relay(1 if late else 0)
+    ensure(lambda item: item[0] != "p")
+    factor = stat_p()
+    warm = factor * cool
+    for j in range(1, n_z):
+        ensure(lambda item: item[0] == "p" and item[1] == j)
+        for k in range(side):
+            partner_blocks(j, k)
+            normalise(j, k, factor)
+        for n in range(n_blocks):
+            run(j * n_blocks + n)
+            if j == n_z - 1 and n > 0:
+                finish(n - 1)
+            else:
+                relay(j + 1 if n >= n_blocks // 2 - 1 else j)
+    finish(n_blocks - 1)
 
     top, total, picked = state
     peak = jnp.max(top, axis=1, keepdims=True)
@@ -483,21 +506,19 @@
         kz = depth // n_z
         bc = min(cols, BLOCK_COLS)
         n_blocks = cols // bc
-        n_early = max(1, n_blocks - n_blocks // 4)
         n_slots = min(n_z * n_blocks, max(2, STREAM_BYTES // (kz * bc * 2)))
         box = group + STAT_ROWS
         n_sends = n_z - 1 + n_z * (2 * side * side - 1)
-        n_acc = max(n_early, min(8, n_blocks))
         accs = [
             pltpu.ACC(q)((slots, TILE), jnp.float32)
-            for _ in range(n_acc)
+            for _ in range(2 * n_blocks)
             for q in range(bc // TILE)
         ]
         vmem = pl.BlockSpec(memory_space=pltpu.VMEM)
         anywhere = pl.BlockSpec(memory_space=pl.ANY)
         gain_rows = gain.reshape(depth // LANES, LANES)
         packed = pl.pallas_call(
-            functools.partial(kernel, n_v, n_b, n_early, accs),
+            functools.partial(kernel, n_v, n_b, accs),
             out_shape=jax.ShapeDtypeStruct((box, LANES), jnp.float32),
             in_specs=[anywhere] * 7,
             out_specs=vmem,

time: 38.9 us -> 37.3 us (0.959)
  Pallas kernels: 38 us -> 36.4 us
    pallas_call x1, Pallas kernels: 36.7 us -> 35.1 us  [local(): pl.pallas_call(functools.partial(kernel, n_v, n_b, accs), out_shape=jax.S...]
where the time goes in v3:
time: 37.3 us; the launch traced here: 37 us
  Pallas kernels  36.4 us (98%)
  between operations  0.64 us (2%)
    pallas_call x1, Pallas kernels, local(): pl.pallas_call(functools.partial(kernel, n_v, n_b, accs), out_shape=jax.S...  35.1 us
    pallas_call x1, Pallas kernels, local(): pl.pallas_call(split, out_shape=(jax.ShapeDtypeStruct((1, group), jnp.flo...  1.32 us

profile of v3, /device:TPU:0, one launch (start us, length us, event | category | flops | bytes accessed | tf_op | source)
XLA Modules:
  0.0 37.0 jit_solution(11540871152049974653)
XLA Ops:
  0.6 35.1 %shard_map.94.all_ref = f32[18,128]{1,0:T(8,128)} custom-call(bf16[16,1024]{1,0:T(8,128)(2,1)} %refs_0_.1, bf16[64,128]{1,0:T(8,128)(2,1)} %bitcast.6, bf16[8192,4096]{1,0:T(8,128)(2,1)} %refs_2_.1, f32[1,16]{1,0:T(1,128)} %bitcast.7, s32[1,64]{1,0:T(1,128)} %bitcast.8, s32[64,128]{1,0:T(8,128)} %refs_5_.1, s32[1,64]{1,0:T(1,128)} %bitcast.9), custom_call_target="tpu_custom_call" | custom-call | tf_op jit(solution)/shard_map/pallas_call | solution.py:520
  35.7 1.3 %shard_map.95 = (f32[1,16]{1,0:T(1,128)}, f32[1,16]{1,0:T(1,128)}, f32[16,128]{1,0:T(8,128)}) custom-call(f32[18,128]{1,0:T(8,128)} %shard_map.94.all_ref), custom_call_target="tpu_custom_call" | custom-call | tf_op jit(solution)/shard_map/pallas_call | solution.py:570

commit v4 on v3

--- a/solution.py
+++ b/solution.py
@@ -129,16 +129,17 @@
 
     mine = place(x, y, c)
 
-    plane = []
-    for dx in range(side):
-        for dy in range(side):
-            for dc in range(2):
-                if dx + dy + dc > 0:
-                    plane.append(((x + dx) % side, (y + dy) % side, (c + dc) % 2))
+    steps = [(dx, dy, dc) for dx in range(side) for dy in range(side) for dc in range(2)]
+    steps.sort(key=lambda d: -2 * ((d[0] > 0) + (d[1] > 0)) - d[2])
+    plane = [
+        ((x + dx) % side, (y + dy) % side, (c + dc) % 2)
+        for dx, dy, dc in steps
+        if dx + dy + dc > 0
+    ]
     order = [flip(z, j) for j in range(n_z)]
 
     barrier = pltpu.get_barrier_semaphore()
-    for j in range(1, n_z):
+    for j in reversed(range(1, n_z)):
         pl.semaphore_signal(
             barrier, inc=1, device_id=device(x, y, order[j], c), device_id_type=MESH
         )
@@ -230,7 +231,7 @@
     same = [(dx, dy) for dx in range(side) for dy in range(side) if dx + dy > 0]
     same.sort(key=lambda d: d[1])
 
-    for j in range(1, n_z):
+    for j in reversed(range(1, n_z)):
         send(
             stat_out.at[0],
             z_stat.at[z],
@@ -463,7 +464,7 @@
     midbox[:group, :] = candidates
     midbox[group : group + 1, :] = top
     midbox[group + 1 : group + 2, :] = total
-    for j in range(1, n_z):
+    for j in reversed(range(1, n_z)):
         send(midbox, lastbox.at[z], u_send.at[j], u_recv.at[z], device(x, y, order[j], c))
     lastbox[z] = midbox[...]
     for j in range(1, n_z):

time: 37.3 us -> 37 us (level)
  no operation moved by 1% of the time
where the time goes in v4:
time: 37 us; the launch traced here: 36.8 us
  Pallas kernels  36.1 us (98%)
  between operations  0.64 us (2%)
    pallas_call x1, Pallas kernels, local(): pl.pallas_call(functools.partial(kernel, n_v, n_b, accs), out_shape=jax.S...  34.8 us
    pallas_call x1, Pallas kernels, local(): pl.pallas_call(split, out_shape=(jax.ShapeDtypeStruct((1, group), jnp.flo...  1.32 us

profile of v4, /device:TPU:0, one launch (start us, length us, event | category | flops | bytes accessed | tf_op | source)
XLA Modules:
  0.0 36.8 jit_solution(3624273400887956345)
XLA Ops:
  0.6 34.8 %shard_map.94.all_ref = f32[18,128]{1,0:T(8,128)} custom-call(bf16[16,1024]{1,0:T(8,128)(2,1)} %refs_0_.1, bf16[64,128]{1,0:T(8,128)(2,1)} %bitcast.6, bf16[8192,4096]{1,0:T(8,128)(2,1)} %refs_2_.1, f32[1,16]{1,0:T(1,128)} %bitcast.7, s32[1,64]{1,0:T(1,128)} %bitcast.8, s32[64,128]{1,0:T(8,128)} %refs_5_.1, s32[1,64]{1,0:T(1,128)} %bitcast.9), custom_call_target="tpu_custom_call" | custom-call | tf_op jit(solution)/shard_map/pallas_call | solution.py:521
  35.4 1.3 %shard_map.95 = (f32[1,16]{1,0:T(1,128)}, f32[1,16]{1,0:T(1,128)}, f32[16,128]{1,0:T(8,128)}) custom-call(f32[18,128]{1,0:T(8,128)} %shard_map.94.all_ref), custom_call_target="tpu_custom_call" | custom-call | tf_op jit(solution)/shard_map/pallas_call | solution.py:571
